TPU v7x, 32 devices: a whole 2x2x4 slice. The times are simulated.
32 devices in a mesh: py: 8 (over y, x, core), px: 4 (over z).
Axes of the slice: x: 2, y: 2, z: 4, core: 2. Of those that a mesh axis runs over, the one named last changes fastest.
Arguments:
- load_terms: float32 [512, 256, 256], P('py', 'px'), may hold values from -6 to 6
- start_values: float32 [512, 256, 256], P('py', 'px'), may hold values from -6 to 6
- reaction_rate: float32 [512, 256, 256], P('py', 'px'), may hold values from 0.1 to 0.9
Outputs:
- corrected: float32 [512, 256, 256], P('py', 'px')
All inputs are finite; a program needn't handle non-finite values.
Results may differ from a plain program's by a relative error of at most 0.00002.
Values sent between devices are 32-bit elements; how exact they have to be, the bound alone decides.
A program may use at most 128 MiB of HBM per device.

v0:
```python
import jax
import jax.numpy as jnp
from jax import lax
from jax.sharding import PartitionSpec as P

RATIO = 4
BEFORE = 2
AFTER = 2
INNER = 7


def extended(value, sides, width):
    for axis, dim in sides:
        size, length = (lax.axis_size(axis), value.shape[dim])
        up = [(i, (i + 1) % size) for i in range(size)]
        down = [(j, i) for i, j in up]
        last = lax.slice_in_dim(value, length - width, length, axis=dim)
        leading = lax.slice_in_dim(value, 0, width, axis=dim)
        before = lax.ppermute(last, axis, up)
        after = lax.ppermute(leading, axis, down)
        value = jnp.concatenate([before, value, after], axis=dim)
    return value


def around_sum(padded):
    inner_y, inner_x = (padded.shape[0] - 2, padded.shape[1] - 2)
    middle_rows = lax.slice_in_dim(padded, 1, 1 + inner_y, axis=0)
    middle_columns = lax.slice_in_dim(padded, 1, 1 + inner_x, axis=1)
    return (
        lax.slice_in_dim(middle_columns, 0, inner_y, axis=0)
        + lax.slice_in_dim(middle_columns, 2, 2 + inner_y, axis=0)
        + lax.slice_in_dim(middle_rows, 0, inner_x, axis=1)
        + lax.slice_in_dim(middle_rows, 2, 2 + inner_x, axis=1)
    )


def relax_once(padded, values, load, mass_here):
    return values + 0.8 * (load + around_sum(padded) - (4.0 + mass_here) * values) / (
        4.0 + mass_here
    )


def block_means(values):
    cut = values.reshape(
        values.shape[0] // RATIO, RATIO, values.shape[1] // RATIO, RATIO, values.shape[2]
    )
    return jnp.mean(cut, axis=(1, 3))


def spread_blocks(values):
    return jnp.repeat(jnp.repeat(values, RATIO, axis=0), RATIO, axis=1)


def inner_part(values):
    return lax.slice_in_dim(
        lax.slice_in_dim(values, 1, values.shape[0] - 1, axis=0), 1, values.shape[1] - 1, axis=1
    )


def per_device(load_terms, start_values, reaction_rate):
    values = start_values
    for sweep in range(BEFORE):
        values = relax_once(
            extended(values, (("py", 0), ("px", 1)), 1), values, load_terms, reaction_rate
        )
    defect = (
        load_terms
        + around_sum(extended(values, (("py", 0), ("px", 1)), 1))
        - (4.0 + reaction_rate) * values
    )
    coarse_load, coarse_mass = (block_means(defect) * RATIO, block_means(reaction_rate) * RATIO)
    coarse_values = 0.8 * coarse_load / (4.0 + coarse_mass)
    load_mass = extended(
        jnp.concatenate([coarse_load, coarse_mass], axis=2), (("py", 0), ("px", 1)), 2
    )
    wide_load, wide_mass = jnp.split(load_mass, 2, axis=2)
    for group in range((INNER - 1) // 2):
        wide_values = extended(coarse_values, (("py", 0), ("px", 1)), 2)
        once = relax_once(
            wide_values, inner_part(wide_values), inner_part(wide_load), inner_part(wide_mass)
        )
        middle = inner_part(once)
        coarse_values = relax_once(once, middle, coarse_load, coarse_mass)
    values = values + spread_blocks(coarse_values)
    for sweep in range(AFTER):
        values = relax_once(
            extended(values, (("py", 0), ("px", 1)), 1), values, load_terms, reaction_rate
        )
    return values


def solution(mesh):
    return jax.shard_map(
        per_device,
        mesh=mesh,
        in_specs=(P("py", "px", None), P("py", "px", None), P("py", "px", None)),
        out_specs=P("py", "px", None),
        check_vma=False,
    )
```

profile of v0, /device:TPU:0, one launch (start us, length us, event | category | flops | bytes accessed | tf_op | source)
XLA Modules:
  0.0 189.7 jit_solution(16462536964365135920)
XLA Ops:
  0.0 0.9 fusion.78
  1.0 3.4 %collective-permute-start.1 = (f32[1,64,256]{2,0,1:T(1,128)S(1)}, f32[1,64,256]{2,0,1:T(1,128)S(1)}, u32[]{:S(2)}, u32[]{:S(2)}) collective-permute-start(f32[1,64,256]{2,0,1:T(1,128)S(1)} %copy.35), channel_id=1, source_target_pairs={{4,0},{8,4},{12,8},{16,12},{20,16},{24,20},{28,24},{0,28},{5,1},{9... | collective-permute-start | bytes 196616 | tf_op jit(solution)/shard_map/ppermute | solution.py:20
  4.5 4.8 %copy.41 = f32[64,64,256]{2,0,1:T(8,128)S(1)} copy(f32[64,64,256]{2,1,0:T(8,128)} %param.4) | data formatting | bytes 8388608 | tf_op args[1]
  9.4 1.6 collective-permute-start.2
  11.0 2.2 %collective-permute-start.3 = (f32[66,1,256]{2,0,1:T(8,128)S(1)}, f32[66,1,256]{2,0,1:T(8,128)S(1)}, u32[]{:S(2)}, u32[]{:S(2)}) collective-permute-start(f32[66,1,256]{2,0,1:T(8,128)S(1)} %get-tuple-element.14), channel_id=1, source_target_pairs={{1,0},{2,1},{3,2},{0,3},{5,4},{6,5},{7,6},{4,7},{9,8},{10,9},{11,1... | collective-permute-start | bytes 202760 | tf_op jit(solution)/shard_map/ppermute | solution.py:20
  13.2 2.9 %collective-permute-done.2 = f32[66,1,256]{2,0,1:T(8,128)S(1)} collective-permute-done((f32[66,1,256]{2,0,1:T(8,128)S(1)}, f32[66,1,256]{2,0,1:T(8,128)S(1)}, u32[]{:S(2)}, u32[]{:S(2)}) %collective-permute-start.2) | collective-permute-done | bytes 67616 | tf_op jit(solution)/shard_map/ppermute | solution.py:19
  16.2 12.4 %fusion.34 = f32[64,64,256]{2,0,1:T(8,128)S(1)} fusion(f32[64,64,256]{2,0,1:T(8,128)S(1)} %copy.41, f32[66,1,256]{2,0,1:T(8,128)S(1)} %collective-permute-done.3, f32[1,64,256]{2,0,1:T(1,128)S(1)} %collective-permute-done.1, f32[1,64,256]{2,0,1:T(1,128)S(1)} %collective-permute-done, f32[66,1,256]{2,0,1:T(8,128)S(1)} %collective-permute-done.2, ...), kind=kLoop, calls=%fused_computation.67 | loop fusion | flops 18874368 | bytes 17043456 | tf_op jit(solution)/shard_map/add | solution.py:38
  28.6 0.1 fusion.77
  28.7 2.6 %collective-permute-start.5 = (f32[1,64,256]{2,0,1:T(1,128)S(1)}, f32[1,64,256]{2,0,1:T(1,128)S(1)}, u32[]{:S(2)}, u32[]{:S(2)}) collective-permute-start(f32[1,64,256]{2,0,1:T(1,128)S(1)} %get-tuple-element.22), channel_id=1, source_target_pairs={{4,0},{8,4},{12,8},{16,12},{20,16},{24,20},{28,24},{0,28},{5,1},{9... | collective-permute-start | bytes 196616 | tf_op jit(solution)/shard_map/ppermute | solution.py:20
  31.4 1.9 %collective-permute-done.4 = f32[1,64,256]{2,0,1:T(1,128)S(1)} collective-permute-done((f32[1,64,256]{2,0,1:T(1,128)S(1)}, f32[1,64,256]{2,0,1:T(1,128)S(1)}, u32[]{:S(2)}, u32[]{:S(2)}) %collective-permute-start.4) | collective-permute-done | bytes 65568 | tf_op jit(solution)/shard_map/ppermute | solution.py:19
  33.3 1.2 collective-permute-start.6
  34.5 2.7 %collective-permute-start.7 = (f32[66,1,256]{2,0,1:T(8,128)S(1)}, f32[66,1,256]{2,0,1:T(8,128)S(1)}, u32[]{:S(2)}, u32[]{:S(2)}) collective-permute-start(f32[66,1,256]{2,0,1:T(8,128)S(1)} %get-tuple-element.12), channel_id=1, source_target_pairs={{1,0},{2,1},{3,2},{0,3},{5,4},{6,5},{7,6},{4,7},{9,8},{10,9},{11,1... | collective-permute-start | bytes 202760 | tf_op jit(solution)/shard_map/ppermute | solution.py:20
  37.2 3.2 %collective-permute-done.6 = f32[66,1,256]{2,0,1:T(8,128)S(1)} collective-permute-done((f32[66,1,256]{2,0,1:T(8,128)S(1)}, f32[66,1,256]{2,0,1:T(8,128)S(1)}, u32[]{:S(2)}, u32[]{:S(2)}) %collective-permute-start.6) | collective-permute-done | bytes 67616 | tf_op jit(solution)/shard_map/ppermute | solution.py:19
  40.4 0.2 collective-permute-done.7
  40.6 12.4 %fusion.26 = f32[64,64,256]{2,0,1:T(8,128)S(1)} fusion(f32[64,64,256]{2,0,1:T(8,128)S(1)} %fusion.34, f32[66,1,256]{2,0,1:T(8,128)S(1)} %collective-permute-done.7, f32[1,64,256]{2,0,1:T(1,128)S(1)} %collective-permute-done.5, f32[1,64,256]{2,0,1:T(1,128)S(1)} %collective-permute-done.4, f32[66,1,256]{2,0,1:T(8,128)S(1)} %collective-permute-done.6, ...), kind=kLoop, calls=%fused_computation.51 | loop fusion | flops 18874368 | bytes 17043456 | tf_op jit(solution)/shard_map/add | solution.py:38
  52.9 0.1 fusion.76
  53.1 2.6 %collective-permute-start.9 = (f32[1,64,256]{2,0,1:T(1,128)S(1)}, f32[1,64,256]{2,0,1:T(1,128)S(1)}, u32[]{:S(2)}, u32[]{:S(2)}) collective-permute-start(f32[1,64,256]{2,0,1:T(1,128)S(1)} %get-tuple-element.20), channel_id=1, source_target_pairs={{4,0},{8,4},{12,8},{16,12},{20,16},{24,20},{28,24},{0,28},{5,1},{9... | collective-permute-start | bytes 196616 | tf_op jit(solution)/shard_map/ppermute | solution.py:20
  55.7 2.6 %collective-permute-done.8 = f32[1,64,256]{2,0,1:T(1,128)S(1)} collective-permute-done((f32[1,64,256]{2,0,1:T(1,128)S(1)}, f32[1,64,256]{2,0,1:T(1,128)S(1)}, u32[]{:S(2)}, u32[]{:S(2)}) %collective-permute-start.8) | collective-permute-done | bytes 65568 | tf_op jit(solution)/shard_map/ppermute | solution.py:19
  58.3 0.6 collective-permute-start.10
  58.9 3.3 %collective-permute-start.11 = (f32[66,1,256]{2,0,1:T(8,128)S(1)}, f32[66,1,256]{2,0,1:T(8,128)S(1)}, u32[]{:S(2)}, u32[]{:S(2)}) collective-permute-start(f32[66,1,256]{2,0,1:T(8,128)S(1)} %get-tuple-element.10), channel_id=1, source_target_pairs={{1,0},{2,1},{3,2},{0,3},{5,4},{6,5},{7,6},{4,7},{9,8},{10,9},{11,1... | collective-permute-start | bytes 202760 | tf_op jit(solution)/shard_map/ppermute | solution.py:20
  62.2 5.2 %reshape.13 = f32[16,4,16,4,256]{4,3,2,1,0:T(4,128)} reshape(f32[64,64,256]{2,1,0:T(8,128)} %param.5) | data formatting | bytes 8388608 | tf_op jit(solution)/shard_map/reshape | solution.py:44
  67.4 3.5 %reduce_sum.19 = f32[16,16,256]{2,1,0:T(8,128)S(1)} reduce(f32[16,4,16,4,256]{4,3,2,1,0:T(4,128)} %reshape.13, f32[]{:T(128)} %constant.7.clone.1), dimensions={1,3}, to_apply=%region_1.0 | reduce | flops 983040 | bytes 4456452 | tf_op jit(solution)/shard_map/reduce_sum | solution.py:47
  71.0 15.0 %fusion.18 = f32[64,64,256]{2,0,1:T(8,128)} fusion(f32[66,1,256]{2,0,1:T(8,128)S(1)} %collective-permute-done.11, f32[1,64,256]{2,0,1:T(1,128)S(1)} %collective-permute-done.9, f32[64,64,256]{2,0,1:T(8,128)} %copy-done.4, f32[1,64,256]{2,0,1:T(1,128)S(1)} %collective-permute-done.8, f32[66,1,256]{2,0,1:T(8,128)S(1)} %collective-permute-done.10, ...), kind=kLoop, calls=%fused_computation.35 | loop fusion | flops 15728640 | bytes 17043456 | tf_op jit(solution)/shard_map/sub | solution.py:67
  86.0 5.2 %reshape.12 = f32[16,4,16,4,256]{4,1,0,3,2:T(4,128)} reshape(f32[64,64,256]{2,0,1:T(8,128)} %fusion.18) | data formatting | bytes 8388608 | tf_op jit(solution)/shard_map/reshape | solution.py:44
  91.2 3.5 %reduce_sum.18 = f32[16,16,256]{2,0,1:T(8,128)S(1)} reduce(f32[16,4,16,4,256]{4,1,0,3,2:T(4,128)} %reshape.12, f32[]{:T(128)} %constant.7.clone.1), dimensions={1,3}, to_apply=%region_0.0 | reduce | flops 983040 | bytes 4456452 | tf_op jit(solution)/shard_map/reduce_sum | solution.py:47
  94.8 0.2 broadcast_multiply_fusion
  95.1 2.6 %collective-permute-start.13 = (f32[2,16,256]{2,0,1:T(2,128)S(1)}, f32[2,16,256]{2,0,1:T(2,128)S(1)}, u32[]{:S(2)}, u32[]{:S(2)}) collective-permute-start(f32[2,16,256]{2,0,1:T(2,128)S(1)} %get-tuple-element.43), channel_id=1, source_target_pairs={{4,0},{8,4},{12,8},{16,12},{20,16},{24,20},{28,24},{0,28},{5,1},{9... | collective-permute-start | bytes 98312 | tf_op jit(solution)/shard_map/ppermute | solution.py:20
  97.8 2.6 %collective-permute-start.17 = (f32[2,16,512]{2,0,1:T(2,128)S(1)}, f32[2,16,512]{2,0,1:T(2,128)S(1)}, u32[]{:S(2)}, u32[]{:S(2)}) collective-permute-start(f32[2,16,512]{2,0,1:T(2,128)S(1)} %get-tuple-element.28), channel_id=1, source_target_pairs={{4,0},{8,4},{12,8},{16,12},{20,16},{24,20},{28,24},{0,28},{5,1},{9... | collective-permute-start | bytes 196616 | tf_op jit(solution)/shard_map/ppermute | solution.py:20
  100.5 3.8 %collective-permute-start.15 = (f32[20,2,256]{2,0,1:T(8,128)S(1)}, f32[20,2,256]{2,0,1:T(8,128)S(1)}, u32[]{:S(2)}, u32[]{:S(2)}) collective-permute-start(f32[20,2,256]{2,0,1:T(8,128)S(1)} %get-tuple-element.34), channel_id=1, source_target_pairs={{1,0},{2,1},{3,2},{0,3},{5,4},{6,5},{7,6},{4,7},{9,8},{10,9},{11,1... | collective-permute-start | bytes 122888 | tf_op jit(solution)/shard_map/ppermute | solution.py:20
  104.5 3.8 %collective-permute-start.19 = (f32[20,2,512]{2,0,1:T(8,128)S(1)}, f32[20,2,512]{2,0,1:T(8,128)S(1)}, u32[]{:S(2)}, u32[]{:S(2)}) collective-permute-start(f32[20,2,512]{2,0,1:T(8,128)S(1)} %get-tuple-element.26), channel_id=1, source_target_pairs={{1,0},{2,1},{3,2},{0,3},{5,4},{6,5},{7,6},{4,7},{9,8},{10,9},{11,1... | collective-permute-start | bytes 245768 | tf_op jit(solution)/shard_map/ppermute | solution.py:20
  108.3 2.5 %collective-permute-done.18 = f32[20,2,512]{2,0,1:T(8,128)S(1)} collective-permute-done((f32[20,2,512]{2,0,1:T(8,128)S(1)}, f32[20,2,512]{2,0,1:T(8,128)S(1)}, u32[]{:S(2)}, u32[]{:S(2)}) %collective-permute-start.18) | collective-permute-done | bytes 81952 | tf_op jit(solution)/shard_map/ppermute | solution.py:19
  110.9 0.4 fusion.57
  111.3 0.3 fusion.73
  111.7 2.6 %collective-permute-start.21 = (f32[2,16,256]{2,0,1:T(2,128)S(1)}, f32[2,16,256]{2,0,1:T(2,128)S(1)}, u32[]{:S(2)}, u32[]{:S(2)}) collective-permute-start(f32[2,16,256]{2,0,1:T(2,128)S(1)} %get-tuple-element.38), channel_id=1, source_target_pairs={{4,0},{8,4},{12,8},{16,12},{20,16},{24,20},{28,24},{0,28},{5,1},{9... | collective-permute-start | bytes 98312 | tf_op jit(solution)/shard_map/ppermute | solution.py:20
  114.3 1.6 collective-permute-done.20
  116.0 3.9 %collective-permute-start.23 = (f32[20,2,256]{2,0,1:T(8,128)S(1)}, f32[20,2,256]{2,0,1:T(8,128)S(1)}, u32[]{:S(2)}, u32[]{:S(2)}) collective-permute-start(f32[20,2,256]{2,0,1:T(8,128)S(1)} %get-tuple-element.32), channel_id=1, source_target_pairs={{1,0},{2,1},{3,2},{0,3},{5,4},{6,5},{7,6},{4,7},{9,8},{10,9},{11,1... | collective-permute-start | bytes 122888 | tf_op jit(solution)/shard_map/ppermute | solution.py:20
  119.9 2.0 %collective-permute-done.22 = f32[20,2,256]{2,0,1:T(8,128)S(1)} collective-permute-done((f32[20,2,256]{2,0,1:T(8,128)S(1)}, f32[20,2,256]{2,0,1:T(8,128)S(1)}, u32[]{:S(2)}, u32[]{:S(2)}) %collective-permute-start.22) | collective-permute-done | bytes 40992 | tf_op jit(solution)/shard_map/ppermute | solution.py:19
  121.9 0.4 fusion.49
  122.4 0.3 fusion.68
  122.7 2.6 %collective-permute-start.25 = (f32[2,16,256]{2,0,1:T(2,128)S(1)}, f32[2,16,256]{2,0,1:T(2,128)S(1)}, u32[]{:S(2)}, u32[]{:S(2)}) collective-permute-start(f32[2,16,256]{2,0,1:T(2,128)S(1)} %get-tuple-element.36), channel_id=1, source_target_pairs={{4,0},{8,4},{12,8},{16,12},{20,16},{24,20},{28,24},{0,28},{5,1},{9... | collective-permute-start | bytes 98312 | tf_op jit(solution)/shard_map/ppermute | solution.py:20
  125.4 1.8 collective-permute-done.24
  127.2 1.1 collective-permute-start.26
  128.3 2.9 %collective-permute-start.27 = (f32[20,2,256]{2,0,1:T(8,128)S(1)}, f32[20,2,256]{2,0,1:T(8,128)S(1)}, u32[]{:S(2)}, u32[]{:S(2)}) collective-permute-start(f32[20,2,256]{2,0,1:T(8,128)S(1)} %get-tuple-element.30), channel_id=1, source_target_pairs={{1,0},{2,1},{3,2},{0,3},{5,4},{6,5},{7,6},{4,7},{9,8},{10,9},{11,1... | collective-permute-start | bytes 122888 | tf_op jit(solution)/shard_map/ppermute | solution.py:20
  131.2 2.1 %collective-permute-done.26 = f32[20,2,256]{2,0,1:T(8,128)S(1)} collective-permute-done((f32[20,2,256]{2,0,1:T(8,128)S(1)}, f32[20,2,256]{2,0,1:T(8,128)S(1)}, u32[]{:S(2)}, u32[]{:S(2)}) %collective-permute-start.26) | collective-permute-done | bytes 40992 | tf_op jit(solution)/shard_map/ppermute | solution.py:19
  133.4 0.4 fusion.42
  133.8 0.3 fusion.63
  134.1 0.2 broadcast_in_dim.6
  134.3 0.4 reshape.14
  134.6 2.8 %bitcast_add_fusion = f32[64,64,256]{2,0,1:T(8,128)S(1)} fusion(f32[64,64,256]{2,0,1:T(8,128)} %copy-done.4, f32[64,16,256]{2,0,1:T(8,128)S(1)} %reshape.14), kind=kLoop, calls=%fused_computation.77 | loop fusion | flops 1048576 | bytes 9437184 | tf_op jit(solution)/shard_map/add | solution.py:84
  137.4 0.1 fusion.75
  137.6 2.6 %collective-permute-start.29 = (f32[1,64,256]{2,0,1:T(1,128)S(1)}, f32[1,64,256]{2,0,1:T(1,128)S(1)}, u32[]{:S(2)}, u32[]{:S(2)}) collective-permute-start(f32[1,64,256]{2,0,1:T(1,128)S(1)} %get-tuple-element.18), channel_id=1, source_target_pairs={{4,0},{8,4},{12,8},{16,12},{20,16},{24,20},{28,24},{0,28},{5,1},{9... | collective-permute-start | bytes 196616 | tf_op jit(solution)/shard_map/ppermute | solution.py:20
  140.2 2.2 %collective-permute-done.28 = f32[1,64,256]{2,0,1:T(1,128)S(1)} collective-permute-done((f32[1,64,256]{2,0,1:T(1,128)S(1)}, f32[1,64,256]{2,0,1:T(1,128)S(1)}, u32[]{:S(2)}, u32[]{:S(2)}) %collective-permute-start.28) | collective-permute-done | bytes 65568 | tf_op jit(solution)/shard_map/ppermute | solution.py:19
  142.5 1.1 collective-permute-start.30
  143.6 2.8 %collective-permute-start.31 = (f32[66,1,256]{2,0,1:T(8,128)S(1)}, f32[66,1,256]{2,0,1:T(8,128)S(1)}, u32[]{:S(2)}, u32[]{:S(2)}) collective-permute-start(f32[66,1,256]{2,0,1:T(8,128)S(1)} %get-tuple-element.8), channel_id=1, source_target_pairs={{1,0},{2,1},{3,2},{0,3},{5,4},{6,5},{7,6},{4,7},{9,8},{10,9},{11,1... | collective-permute-start | bytes 202760 | tf_op jit(solution)/shard_map/ppermute | solution.py:20
  146.4 3.0 %collective-permute-done.30 = f32[66,1,256]{2,0,1:T(8,128)S(1)} collective-permute-done((f32[66,1,256]{2,0,1:T(8,128)S(1)}, f32[66,1,256]{2,0,1:T(8,128)S(1)}, u32[]{:S(2)}, u32[]{:S(2)}) %collective-permute-start.30) | collective-permute-done | bytes 67616 | tf_op jit(solution)/shard_map/ppermute | solution.py:19
  149.4 12.4 %fusion.13 = f32[64,64,256]{2,0,1:T(8,128)S(1)} fusion(f32[64,64,256]{2,0,1:T(8,128)S(1)} %bitcast_add_fusion, f32[66,1,256]{2,0,1:T(8,128)S(1)} %collective-permute-done.31, f32[1,64,256]{2,0,1:T(1,128)S(1)} %collective-permute-done.29, f32[1,64,256]{2,0,1:T(1,128)S(1)} %collective-permute-done.28, f32[66,1,256]{2,0,1:T(8,128)S(1)} %collective-permute-done.30, ...), kind=kLoop, calls=%fused_computation.22 | loop fusion | flops 18874368 | bytes 17043456 | tf_op jit(solution)/shard_map/add | solution.py:38
  161.9 0.1 fusion.74
  162.0 2.6 %collective-permute-start.33 = (f32[1,64,256]{2,0,1:T(1,128)S(1)}, f32[1,64,256]{2,0,1:T(1,128)S(1)}, u32[]{:S(2)}, u32[]{:S(2)}) collective-permute-start(f32[1,64,256]{2,0,1:T(1,128)S(1)} %get-tuple-element.16), channel_id=1, source_target_pairs={{4,0},{8,4},{12,8},{16,12},{20,16},{24,20},{28,24},{0,28},{5,1},{9... | collective-permute-start | bytes 196616 | tf_op jit(solution)/shard_map/ppermute | solution.py:20
  164.6 1.9 %collective-permute-done.32 = f32[1,64,256]{2,0,1:T(1,128)S(1)} collective-permute-done((f32[1,64,256]{2,0,1:T(1,128)S(1)}, f32[1,64,256]{2,0,1:T(1,128)S(1)}, u32[]{:S(2)}, u32[]{:S(2)}) %collective-permute-start.32) | collective-permute-done | bytes 65568 | tf_op jit(solution)/shard_map/ppermute | solution.py:19
  166.6 0.9 collective-permute-start.34
  167.5 3.0 %collective-permute-start.35 = (f32[66,1,256]{2,0,1:T(8,128)S(1)}, f32[66,1,256]{2,0,1:T(8,128)S(1)}, u32[]{:S(2)}, u32[]{:S(2)}) collective-permute-start(f32[66,1,256]{2,0,1:T(8,128)S(1)} %get-tuple-element.6), channel_id=1, source_target_pairs={{1,0},{2,1},{3,2},{0,3},{5,4},{6,5},{7,6},{4,7},{9,8},{10,9},{11,1... | collective-permute-start | bytes 202760 | tf_op jit(solution)/shard_map/ppermute | solution.py:20
  170.5 2.4 %collective-permute-done.34 = f32[66,1,256]{2,0,1:T(8,128)S(1)} collective-permute-done((f32[66,1,256]{2,0,1:T(8,128)S(1)}, f32[66,1,256]{2,0,1:T(8,128)S(1)}, u32[]{:S(2)}, u32[]{:S(2)}) %collective-permute-start.34) | collective-permute-done | bytes 67616 | tf_op jit(solution)/shard_map/ppermute | solution.py:19
  172.9 12.4 %fusion.5 = f32[64,64,256]{2,0,1:T(8,128)S(1)} fusion(f32[64,64,256]{2,0,1:T(8,128)S(1)} %fusion.13, f32[66,1,256]{2,0,1:T(8,128)S(1)} %collective-permute-done.35, f32[1,64,256]{2,0,1:T(1,128)S(1)} %collective-permute-done.33, f32[1,64,256]{2,0,1:T(1,128)S(1)} %collective-permute-done.32, f32[66,1,256]{2,0,1:T(8,128)S(1)} %collective-permute-done.34, ...), kind=kLoop, calls=%fused_computation.6 | loop fusion | flops 18874368 | bytes 17043456 | tf_op jit(solution)/shard_map/add | solution.py:38
  185.3 4.4 %copy.47 = f32[64,64,256]{2,1,0:T(8,128)} copy(f32[64,64,256]{2,0,1:T(8,128)S(1)} %fusion.5) | data formatting | bytes 8388608 | tf_op jit(solution)/shard_map/add | solution.py:38
  (62 shorter events, 1.5 us)
Async XLA Ops:
  1.0 8.4 %collective-permute-start.1 = (f32[1,64,256]{2,0,1:T(1,128)S(1)}, f32[1,64,256]{2,0,1:T(1,128)S(1)}, u32[]{:S(2)}, u32[]{:S(2)}) collective-permute-start(f32[1,64,256]{2,0,1:T(1,128)S(1)} %copy.35), channel_id=1, source_target_pairs={{4,0},{8,4},{12,8},{16,12},{20,16},{24,20},{28,24},{0,28},{5,1},{9... | collective-permute-start | bytes 196616 | tf_op jit(solution)/shard_map/ppermute | solution.py:20
  4.4 4.9 %collective-permute-start = (f32[1,64,256]{2,0,1:T(1,128)S(1)}, f32[1,64,256]{2,0,1:T(1,128)S(1)}, u32[]{:S(2)}, u32[]{:S(2)}) collective-permute-start(f32[1,64,256]{2,0,1:T(1,128)S(1)} %copy.33), channel_id=1, source_target_pairs={{0,4},{4,8},{8,12},{12,16},{16,20},{20,24},{24,28},{28,0},{1,5},{5... | collective-permute-start | bytes 196616 | tf_op jit(solution)/shard_map/ppermute | solution.py:19
  4.5 11.7 %copy-start.2 = (f32[64,64,256]{2,1,0:T(8,128)S(1)}, f32[64,64,256]{2,1,0:T(8,128)}, u32[]{:S(2)}) copy-start(f32[64,64,256]{2,1,0:T(8,128)} %param.3) | copy-start | bytes 12582916
  9.3 6.9 %copy-start = (f32[64,64,256]{2,1,0:T(8,128)S(1)}, f32[64,64,256]{2,1,0:T(8,128)}, u32[]{:S(2)}) copy-start(f32[64,64,256]{2,1,0:T(8,128)} %param.5) | copy-start | bytes 12582916
  9.4 6.7 %collective-permute-start.2 = (f32[66,1,256]{2,0,1:T(8,128)S(1)}, f32[66,1,256]{2,0,1:T(8,128)S(1)}, u32[]{:S(2)}, u32[]{:S(2)}) collective-permute-start(f32[66,1,256]{2,0,1:T(8,128)S(1)} %get-tuple-element.13), channel_id=1, source_target_pairs={{0,1},{1,2},{2,3},{3,0},{4,5},{5,6},{6,7},{7,4},{8,9},{9,10},{10,1... | collective-permute-start | bytes 202760 | tf_op jit(solution)/shard_map/ppermute | solution.py:19
  11.0 5.2 %collective-permute-start.3 = (f32[66,1,256]{2,0,1:T(8,128)S(1)}, f32[66,1,256]{2,0,1:T(8,128)S(1)}, u32[]{:S(2)}, u32[]{:S(2)}) collective-permute-start(f32[66,1,256]{2,0,1:T(8,128)S(1)} %get-tuple-element.14), channel_id=1, source_target_pairs={{1,0},{2,1},{3,2},{0,3},{5,4},{6,5},{7,6},{4,7},{9,8},{10,9},{11,1... | collective-permute-start | bytes 202760 | tf_op jit(solution)/shard_map/ppermute | solution.py:20
  28.7 4.6 %collective-permute-start.4 = (f32[1,64,256]{2,0,1:T(1,128)S(1)}, f32[1,64,256]{2,0,1:T(1,128)S(1)}, u32[]{:S(2)}, u32[]{:S(2)}) collective-permute-start(f32[1,64,256]{2,0,1:T(1,128)S(1)} %get-tuple-element.21), channel_id=1, source_target_pairs={{0,4},{4,8},{8,12},{12,16},{16,20},{20,24},{24,28},{28,0},{1,5},{5... | collective-permute-start | bytes 196616 | tf_op jit(solution)/shard_map/ppermute | solution.py:19
  28.7 4.6 %collective-permute-start.5 = (f32[1,64,256]{2,0,1:T(1,128)S(1)}, f32[1,64,256]{2,0,1:T(1,128)S(1)}, u32[]{:S(2)}, u32[]{:S(2)}) collective-permute-start(f32[1,64,256]{2,0,1:T(1,128)S(1)} %get-tuple-element.22), channel_id=1, source_target_pairs={{4,0},{8,4},{12,8},{16,12},{20,16},{24,20},{28,24},{0,28},{5,1},{9... | collective-permute-start | bytes 196616 | tf_op jit(solution)/shard_map/ppermute | solution.py:20
  33.3 7.0 %collective-permute-start.6 = (f32[66,1,256]{2,0,1:T(8,128)S(1)}, f32[66,1,256]{2,0,1:T(8,128)S(1)}, u32[]{:S(2)}, u32[]{:S(2)}) collective-permute-start(f32[66,1,256]{2,0,1:T(8,128)S(1)} %get-tuple-element.11), channel_id=1, source_target_pairs={{0,1},{1,2},{2,3},{3,0},{4,5},{5,6},{6,7},{7,4},{8,9},{9,10},{10,1... | collective-permute-start | bytes 202760 | tf_op jit(solution)/shard_map/ppermute | solution.py:19
  34.5 6.0 %collective-permute-start.7 = (f32[66,1,256]{2,0,1:T(8,128)S(1)}, f32[66,1,256]{2,0,1:T(8,128)S(1)}, u32[]{:S(2)}, u32[]{:S(2)}) collective-permute-start(f32[66,1,256]{2,0,1:T(8,128)S(1)} %get-tuple-element.12), channel_id=1, source_target_pairs={{1,0},{2,1},{3,2},{0,3},{5,4},{6,5},{7,6},{4,7},{9,8},{10,9},{11,1... | collective-permute-start | bytes 202760 | tf_op jit(solution)/shard_map/ppermute | solution.py:20
  52.9 5.4 %copy-start.4 = (f32[64,64,256]{2,0,1:T(8,128)}, f32[64,64,256]{2,0,1:T(8,128)S(1)}, u32[]{:S(2)}) copy-start(f32[64,64,256]{2,0,1:T(8,128)S(1)} %fusion.26) | copy-start | bytes 12582916
  53.0 5.3 %collective-permute-start.8 = (f32[1,64,256]{2,0,1:T(1,128)S(1)}, f32[1,64,256]{2,0,1:T(1,128)S(1)}, u32[]{:S(2)}, u32[]{:S(2)}) collective-permute-start(f32[1,64,256]{2,0,1:T(1,128)S(1)} %get-tuple-element.19), channel_id=1, source_target_pairs={{0,4},{4,8},{8,12},{12,16},{16,20},{20,24},{24,28},{28,0},{1,5},{5... | collective-permute-start | bytes 196616 | tf_op jit(solution)/shard_map/ppermute | solution.py:19
  53.1 5.2 %collective-permute-start.9 = (f32[1,64,256]{2,0,1:T(1,128)S(1)}, f32[1,64,256]{2,0,1:T(1,128)S(1)}, u32[]{:S(2)}, u32[]{:S(2)}) collective-permute-start(f32[1,64,256]{2,0,1:T(1,128)S(1)} %get-tuple-element.20), channel_id=1, source_target_pairs={{4,0},{8,4},{12,8},{16,12},{20,16},{24,20},{28,24},{0,28},{5,1},{9... | collective-permute-start | bytes 196616 | tf_op jit(solution)/shard_map/ppermute | solution.py:20
  58.3 12.6 %collective-permute-start.10 = (f32[66,1,256]{2,0,1:T(8,128)S(1)}, f32[66,1,256]{2,0,1:T(8,128)S(1)}, u32[]{:S(2)}, u32[]{:S(2)}) collective-permute-start(f32[66,1,256]{2,0,1:T(8,128)S(1)} %get-tuple-element.9), channel_id=1, source_target_pairs={{0,1},{1,2},{2,3},{3,0},{4,5},{5,6},{6,7},{7,4},{8,9},{9,10},{10,1... | collective-permute-start | bytes 202760 | tf_op jit(solution)/shard_map/ppermute | solution.py:19
  58.9 12.0 %collective-permute-start.11 = (f32[66,1,256]{2,0,1:T(8,128)S(1)}, f32[66,1,256]{2,0,1:T(8,128)S(1)}, u32[]{:S(2)}, u32[]{:S(2)}) collective-permute-start(f32[66,1,256]{2,0,1:T(8,128)S(1)} %get-tuple-element.10), channel_id=1, source_target_pairs={{1,0},{2,1},{3,2},{0,3},{5,4},{6,5},{7,6},{4,7},{9,8},{10,9},{11,1... | collective-permute-start | bytes 202760 | tf_op jit(solution)/shard_map/ppermute | solution.py:20
  95.0 5.4 %collective-permute-start.12 = (f32[2,16,256]{2,0,1:T(2,128)S(1)}, f32[2,16,256]{2,0,1:T(2,128)S(1)}, u32[]{:S(2)}, u32[]{:S(2)}) collective-permute-start(f32[2,16,256]{2,0,1:T(2,128)S(1)} %get-tuple-element.42), channel_id=1, source_target_pairs={{0,4},{4,8},{8,12},{12,16},{16,20},{20,24},{24,28},{28,0},{1,5},{5... | collective-permute-start | bytes 98312 | tf_op jit(solution)/shard_map/ppermute | solution.py:19
  95.1 5.4 %collective-permute-start.13 = (f32[2,16,256]{2,0,1:T(2,128)S(1)}, f32[2,16,256]{2,0,1:T(2,128)S(1)}, u32[]{:S(2)}, u32[]{:S(2)}) collective-permute-start(f32[2,16,256]{2,0,1:T(2,128)S(1)} %get-tuple-element.43), channel_id=1, source_target_pairs={{4,0},{8,4},{12,8},{16,12},{20,16},{24,20},{28,24},{0,28},{5,1},{9... | collective-permute-start | bytes 98312 | tf_op jit(solution)/shard_map/ppermute | solution.py:20
  97.7 6.6 %collective-permute-start.16 = (f32[2,16,512]{2,0,1:T(2,128)S(1)}, f32[2,16,512]{2,0,1:T(2,128)S(1)}, u32[]{:S(2)}, u32[]{:S(2)}) collective-permute-start(f32[2,16,512]{2,0,1:T(2,128)S(1)} %get-tuple-element.27), channel_id=1, source_target_pairs={{0,4},{4,8},{8,12},{12,16},{16,20},{20,24},{24,28},{28,0},{1,5},{5... | collective-permute-start | bytes 196616 | tf_op jit(solution)/shard_map/ppermute | solution.py:19
  97.8 6.5 %collective-permute-start.17 = (f32[2,16,512]{2,0,1:T(2,128)S(1)}, f32[2,16,512]{2,0,1:T(2,128)S(1)}, u32[]{:S(2)}, u32[]{:S(2)}) collective-permute-start(f32[2,16,512]{2,0,1:T(2,128)S(1)} %get-tuple-element.28), channel_id=1, source_target_pairs={{4,0},{8,4},{12,8},{16,12},{20,16},{24,20},{28,24},{0,28},{5,1},{9... | collective-permute-start | bytes 196616 | tf_op jit(solution)/shard_map/ppermute | solution.py:20
  100.5 7.8 %collective-permute-start.14 = (f32[20,2,256]{2,0,1:T(8,128)S(1)}, f32[20,2,256]{2,0,1:T(8,128)S(1)}, u32[]{:S(2)}, u32[]{:S(2)}) collective-permute-start(f32[20,2,256]{2,0,1:T(8,128)S(1)} %get-tuple-element.33), channel_id=1, source_target_pairs={{0,1},{1,2},{2,3},{3,0},{4,5},{5,6},{6,7},{7,4},{8,9},{9,10},{10,1... | collective-permute-start | bytes 122888 | tf_op jit(solution)/shard_map/ppermute | solution.py:19
  100.5 7.7 %collective-permute-start.15 = (f32[20,2,256]{2,0,1:T(8,128)S(1)}, f32[20,2,256]{2,0,1:T(8,128)S(1)}, u32[]{:S(2)}, u32[]{:S(2)}) collective-permute-start(f32[20,2,256]{2,0,1:T(8,128)S(1)} %get-tuple-element.34), channel_id=1, source_target_pairs={{1,0},{2,1},{3,2},{0,3},{5,4},{6,5},{7,6},{4,7},{9,8},{10,9},{11,1... | collective-permute-start | bytes 122888 | tf_op jit(solution)/shard_map/ppermute | solution.py:20
  104.4 6.5 %collective-permute-start.18 = (f32[20,2,512]{2,0,1:T(8,128)S(1)}, f32[20,2,512]{2,0,1:T(8,128)S(1)}, u32[]{:S(2)}, u32[]{:S(2)}) collective-permute-start(f32[20,2,512]{2,0,1:T(8,128)S(1)} %get-tuple-element.25), channel_id=1, source_target_pairs={{0,1},{1,2},{2,3},{3,0},{4,5},{5,6},{6,7},{7,4},{8,9},{9,10},{10,1... | collective-permute-start | bytes 245768 | tf_op jit(solution)/shard_map/ppermute | solution.py:19
  104.5 6.4 %collective-permute-start.19 = (f32[20,2,512]{2,0,1:T(8,128)S(1)}, f32[20,2,512]{2,0,1:T(8,128)S(1)}, u32[]{:S(2)}, u32[]{:S(2)}) collective-permute-start(f32[20,2,512]{2,0,1:T(8,128)S(1)} %get-tuple-element.26), channel_id=1, source_target_pairs={{1,0},{2,1},{3,2},{0,3},{5,4},{6,5},{7,6},{4,7},{9,8},{10,9},{11,1... | collective-permute-start | bytes 245768 | tf_op jit(solution)/shard_map/ppermute | solution.py:20
  111.6 4.3 %collective-permute-start.20 = (f32[2,16,256]{2,0,1:T(2,128)S(1)}, f32[2,16,256]{2,0,1:T(2,128)S(1)}, u32[]{:S(2)}, u32[]{:S(2)}) collective-permute-start(f32[2,16,256]{2,0,1:T(2,128)S(1)} %get-tuple-element.37), channel_id=1, source_target_pairs={{0,4},{4,8},{8,12},{12,16},{16,20},{20,24},{24,28},{28,0},{1,5},{5... | collective-permute-start | bytes 98312 | tf_op jit(solution)/shard_map/ppermute | solution.py:19
  111.7 4.2 %collective-permute-start.21 = (f32[2,16,256]{2,0,1:T(2,128)S(1)}, f32[2,16,256]{2,0,1:T(2,128)S(1)}, u32[]{:S(2)}, u32[]{:S(2)}) collective-permute-start(f32[2,16,256]{2,0,1:T(2,128)S(1)} %get-tuple-element.38), channel_id=1, source_target_pairs={{4,0},{8,4},{12,8},{16,12},{20,16},{24,20},{28,24},{0,28},{5,1},{9... | collective-permute-start | bytes 98312 | tf_op jit(solution)/shard_map/ppermute | solution.py:20
  115.9 5.9 %collective-permute-start.22 = (f32[20,2,256]{2,0,1:T(8,128)S(1)}, f32[20,2,256]{2,0,1:T(8,128)S(1)}, u32[]{:S(2)}, u32[]{:S(2)}) collective-permute-start(f32[20,2,256]{2,0,1:T(8,128)S(1)} %get-tuple-element.31), channel_id=1, source_target_pairs={{0,1},{1,2},{2,3},{3,0},{4,5},{5,6},{6,7},{7,4},{8,9},{9,10},{10,1... | collective-permute-start | bytes 122888 | tf_op jit(solution)/shard_map/ppermute | solution.py:19
  116.0 5.9 %collective-permute-start.23 = (f32[20,2,256]{2,0,1:T(8,128)S(1)}, f32[20,2,256]{2,0,1:T(8,128)S(1)}, u32[]{:S(2)}, u32[]{:S(2)}) collective-permute-start(f32[20,2,256]{2,0,1:T(8,128)S(1)} %get-tuple-element.32), channel_id=1, source_target_pairs={{1,0},{2,1},{3,2},{0,3},{5,4},{6,5},{7,6},{4,7},{9,8},{10,9},{11,1... | collective-permute-start | bytes 122888 | tf_op jit(solution)/shard_map/ppermute | solution.py:20
  122.7 4.5 %collective-permute-start.24 = (f32[2,16,256]{2,0,1:T(2,128)S(1)}, f32[2,16,256]{2,0,1:T(2,128)S(1)}, u32[]{:S(2)}, u32[]{:S(2)}) collective-permute-start(f32[2,16,256]{2,0,1:T(2,128)S(1)} %get-tuple-element.35), channel_id=1, source_target_pairs={{0,4},{4,8},{8,12},{12,16},{16,20},{20,24},{24,28},{28,0},{1,5},{5... | collective-permute-start | bytes 98312 | tf_op jit(solution)/shard_map/ppermute | solution.py:19
  122.7 4.4 %collective-permute-start.25 = (f32[2,16,256]{2,0,1:T(2,128)S(1)}, f32[2,16,256]{2,0,1:T(2,128)S(1)}, u32[]{:S(2)}, u32[]{:S(2)}) collective-permute-start(f32[2,16,256]{2,0,1:T(2,128)S(1)} %get-tuple-element.36), channel_id=1, source_target_pairs={{4,0},{8,4},{12,8},{16,12},{20,16},{24,20},{28,24},{0,28},{5,1},{9... | collective-permute-start | bytes 98312 | tf_op jit(solution)/shard_map/ppermute | solution.py:20
  127.2 6.1 %collective-permute-start.26 = (f32[20,2,256]{2,0,1:T(8,128)S(1)}, f32[20,2,256]{2,0,1:T(8,128)S(1)}, u32[]{:S(2)}, u32[]{:S(2)}) collective-permute-start(f32[20,2,256]{2,0,1:T(8,128)S(1)} %get-tuple-element.29), channel_id=1, source_target_pairs={{0,1},{1,2},{2,3},{3,0},{4,5},{5,6},{6,7},{7,4},{8,9},{9,10},{10,1... | collective-permute-start | bytes 122888 | tf_op jit(solution)/shard_map/ppermute | solution.py:19
  128.3 5.0 %collective-permute-start.27 = (f32[20,2,256]{2,0,1:T(8,128)S(1)}, f32[20,2,256]{2,0,1:T(8,128)S(1)}, u32[]{:S(2)}, u32[]{:S(2)}) collective-permute-start(f32[20,2,256]{2,0,1:T(8,128)S(1)} %get-tuple-element.30), channel_id=1, source_target_pairs={{1,0},{2,1},{3,2},{0,3},{5,4},{6,5},{7,6},{4,7},{9,8},{10,9},{11,1... | collective-permute-start | bytes 122888 | tf_op jit(solution)/shard_map/ppermute | solution.py:20
  134.6 14.8 %copy-start.3 = (f32[64,64,256]{2,1,0:T(8,128)S(1)}, f32[64,64,256]{2,1,0:T(8,128)}, u32[]{:S(2)}) copy-start(f32[64,64,256]{2,1,0:T(8,128)} %param.3) | copy-start | bytes 12582916
  137.4 12.0 %copy-start.1 = (f32[64,64,256]{2,1,0:T(8,128)S(1)}, f32[64,64,256]{2,1,0:T(8,128)}, u32[]{:S(2)}) copy-start(f32[64,64,256]{2,1,0:T(8,128)} %param.5) | copy-start | bytes 12582916
  137.5 4.9 %collective-permute-start.28 = (f32[1,64,256]{2,0,1:T(1,128)S(1)}, f32[1,64,256]{2,0,1:T(1,128)S(1)}, u32[]{:S(2)}, u32[]{:S(2)}) collective-permute-start(f32[1,64,256]{2,0,1:T(1,128)S(1)} %get-tuple-element.17), channel_id=1, source_target_pairs={{0,4},{4,8},{8,12},{12,16},{16,20},{20,24},{24,28},{28,0},{1,5},{5... | collective-permute-start | bytes 196616 | tf_op jit(solution)/shard_map/ppermute | solution.py:19
  137.6 4.8 %collective-permute-start.29 = (f32[1,64,256]{2,0,1:T(1,128)S(1)}, f32[1,64,256]{2,0,1:T(1,128)S(1)}, u32[]{:S(2)}, u32[]{:S(2)}) collective-permute-start(f32[1,64,256]{2,0,1:T(1,128)S(1)} %get-tuple-element.18), channel_id=1, source_target_pairs={{4,0},{8,4},{12,8},{16,12},{20,16},{24,20},{28,24},{0,28},{5,1},{9... | collective-permute-start | bytes 196616 | tf_op jit(solution)/shard_map/ppermute | solution.py:20
  142.5 7.0 %collective-permute-start.30 = (f32[66,1,256]{2,0,1:T(8,128)S(1)}, f32[66,1,256]{2,0,1:T(8,128)S(1)}, u32[]{:S(2)}, u32[]{:S(2)}) collective-permute-start(f32[66,1,256]{2,0,1:T(8,128)S(1)} %get-tuple-element.7), channel_id=1, source_target_pairs={{0,1},{1,2},{2,3},{3,0},{4,5},{5,6},{6,7},{7,4},{8,9},{9,10},{10,1... | collective-permute-start | bytes 202760 | tf_op jit(solution)/shard_map/ppermute | solution.py:19
  143.6 5.9 %collective-permute-start.31 = (f32[66,1,256]{2,0,1:T(8,128)S(1)}, f32[66,1,256]{2,0,1:T(8,128)S(1)}, u32[]{:S(2)}, u32[]{:S(2)}) collective-permute-start(f32[66,1,256]{2,0,1:T(8,128)S(1)} %get-tuple-element.8), channel_id=1, source_target_pairs={{1,0},{2,1},{3,2},{0,3},{5,4},{6,5},{7,6},{4,7},{9,8},{10,9},{11,1... | collective-permute-start | bytes 202760 | tf_op jit(solution)/shard_map/ppermute | solution.py:20
  162.0 4.6 %collective-permute-start.32 = (f32[1,64,256]{2,0,1:T(1,128)S(1)}, f32[1,64,256]{2,0,1:T(1,128)S(1)}, u32[]{:S(2)}, u32[]{:S(2)}) collective-permute-start(f32[1,64,256]{2,0,1:T(1,128)S(1)} %get-tuple-element.15), channel_id=1, source_target_pairs={{0,4},{4,8},{8,12},{12,16},{16,20},{20,24},{24,28},{28,0},{1,5},{5... | collective-permute-start | bytes 196616 | tf_op jit(solution)/shard_map/ppermute | solution.py:19
  162.0 4.6 %collective-permute-start.33 = (f32[1,64,256]{2,0,1:T(1,128)S(1)}, f32[1,64,256]{2,0,1:T(1,128)S(1)}, u32[]{:S(2)}, u32[]{:S(2)}) collective-permute-start(f32[1,64,256]{2,0,1:T(1,128)S(1)} %get-tuple-element.16), channel_id=1, source_target_pairs={{4,0},{8,4},{12,8},{16,12},{20,16},{24,20},{28,24},{0,28},{5,1},{9... | collective-permute-start | bytes 196616 | tf_op jit(solution)/shard_map/ppermute | solution.py:20
  166.6 6.3 %collective-permute-start.34 = (f32[66,1,256]{2,0,1:T(8,128)S(1)}, f32[66,1,256]{2,0,1:T(8,128)S(1)}, u32[]{:S(2)}, u32[]{:S(2)}) collective-permute-start(f32[66,1,256]{2,0,1:T(8,128)S(1)} %get-tuple-element.5), channel_id=1, source_target_pairs={{0,1},{1,2},{2,3},{3,0},{4,5},{5,6},{6,7},{7,4},{8,9},{9,10},{10,1... | collective-permute-start | bytes 202760 | tf_op jit(solution)/shard_map/ppermute | solution.py:19
  167.5 5.4 %collective-permute-start.35 = (f32[66,1,256]{2,0,1:T(8,128)S(1)}, f32[66,1,256]{2,0,1:T(8,128)S(1)}, u32[]{:S(2)}, u32[]{:S(2)}) collective-permute-start(f32[66,1,256]{2,0,1:T(8,128)S(1)} %get-tuple-element.6), channel_id=1, source_target_pairs={{1,0},{2,1},{3,2},{0,3},{5,4},{6,5},{7,6},{4,7},{9,8},{10,9},{11,1... | collective-permute-start | bytes 202760 | tf_op jit(solution)/shard_map/ppermute | solution.py:20
where the time goes:
time: 190 us
  other arithmetic  77.1 us (41%)
  starting transfers between devices  60.1 us (32%)
  waiting for transfers between devices  30.4 us (16%)
  local copies, waits for them, and re-layouts  21.7 us (11%)
    ppermute x18, starting transfers between devices, extended(): after = lax.ppermute(leading, axis, down)  52.9 us
    add x10, other arithmetic, relax_once(): values + 0.8 * (load + around_sum(padded) - (4.0 + mass_here) * values) /...  51.6 us
    ppermute x18, waiting for transfers between devices, extended(): before = lax.ppermute(last, axis, up)  30.1 us
    sub x1, other arithmetic, per_device(): load_terms + around_sum(extended(values, (('py', 0), ('px', 1)), 1))  15 us
    reshape x2, local copies, waits for them, and re-layouts, block_means(): values.reshape(values.shape[0] // RATIO, RATIO, values.shape[1] // RATIO,...  10.4 us
    ppermute x18, starting transfers between devices, extended(): before = lax.ppermute(last, axis, up)  7.18 us
    reduce_sum x2, other arithmetic, block_means(): return jnp.mean(cut, axis=(1, 3))  7.09 us
    unnamed x11, local copies, waits for them, and re-layouts  4.8 us
  transfers between devices with their start and end apart: 36, of which 15 were waited for; matrix products, arithmetic and copies ran while one was open for 7% of the time, Pallas kernels for 0%

commit v1 on v0

v1 whole, which is shorter than its diff:
```python
import functools

import jax
import jax.numpy as jnp
from jax import lax
from jax.experimental import pallas as pl
from jax.experimental.pallas import tpu as pltpu
from jax.sharding import PartitionSpec as P

RATIO = 4
BEFORE = 2
AFTER = 2
INNER = 7
PAD = 8
HU = 2
HL = 1
HC = INNER
LANES = 128
DIAGONALS = ((-1, -1), (-1, 1), (1, -1), (1, 1))


def span(step, halo, size, depth):
    if step == 0:
        return halo, halo, size
    if step < 0:
        return halo, halo + size, depth
    return halo + size - depth, halo - depth, depth


def kernel(
    sizes, load_hbm, start_hbm, mass_hbm, out_hbm,
    u0, u1, u2, ld, ms, wt, cl, cm, cw, cva, cvb,
    pack0, pack1, land0, land1, tmp, spread, in_sem, out_sem, send_sem, recv_sem,
):
    ny, nx, members, n_py, n_px = sizes
    cy, cx = ny // RATIO, nx // RATIO
    wide = nx + 2 * PAD
    cwide = cx + 2 * PAD
    halves = [pl.ds(i, LANES) for i in range(0, members, LANES)]
    iy, ix = lax.axis_index("py"), lax.axis_index("px")

    def device(dy, dx):
        return (lax.rem(iy + dy + n_py, n_py), lax.rem(ix + dx + n_px, n_px))

    middle = pl.ds(PAD, nx)
    loads = [
        pltpu.make_async_copy(start_hbm, u0.at[pl.ds(HU, ny), middle], in_sem.at[0]),
        pltpu.make_async_copy(load_hbm, ld.at[pl.ds(HL, ny), middle], in_sem.at[1]),
        pltpu.make_async_copy(mass_hbm, ms.at[pl.ds(HL, ny), middle], in_sem.at[2]),
    ]
    for copy in loads:
        copy.start()

    barrier = pltpu.get_barrier_semaphore()
    around = ((-1, 0), (1, 0), (0, -1), (0, 1)) + DIAGONALS
    for dy, dx in around:
        pl.semaphore_signal(
            barrier, inc=1, device_id=device(dy, dx), device_id_type=pl.DeviceIdType.MESH
        )
    pl.semaphore_wait(barrier, len(around))

    count = [0]

    def send(src, dst, dy, dx):
        at = count[0]
        count[0] += 1
        copy = pltpu.make_async_remote_copy(
            src_ref=src, dst_ref=dst, send_sem=send_sem.at[at], recv_sem=recv_sem.at[at],
            device_id=device(dy, dx), device_id_type=pl.DeviceIdType.MESH,
        )
        copy.start()
        return copy

    def send_block(ref, dy, dx, halo, rows, columns, depth):
        sy, ty, ly = span(dy, halo, rows, depth)
        sx, tx, lx = span(dx, PAD, columns, PAD)
        return send(
            ref.at[pl.ds(sy, ly), pl.ds(sx, lx)], ref.at[pl.ds(ty, ly), pl.ds(tx, lx)], dy, dx
        )

    def pack_column(buf, side, at, ref, halo, column):
        def group(g, carry):
            for j in range(8):
                buf[side, at, g, j : j + 1, :] = ref[halo + g * 8 + j, column : column + 1, :]
            return carry

        lax.fori_loop(0, ny // 8, group, 0)

    def unpack_column(buf, side, at, ref, halo, column):
        def group(g, carry):
            for j in range(8):
                ref[halo + g * 8 + j, column : column + 1, :] = buf[side, at, g, j : j + 1, :]
            return carry

        lax.fori_loop(0, ny // 8, group, 0)

    first, last = PAD, PAD + nx - 1
    started = []
    loads[0].wait()
    for k in range(2):
        pack_column(pack0, 0, k, u0, HU, first + k)
        pack_column(pack0, 1, k, u0, HU, last - k)
    for dy in (-1, 1):
        started.append(send_block(u0, dy, 0, HU, ny, nx, HU))
    for dy, dx in DIAGONALS:
        started.append(send_block(u0, dy, dx, HU, ny, nx, 1))
    loads[1].wait()
    pack_column(pack0, 0, 2, ld, HL, first)
    pack_column(pack0, 1, 2, ld, HL, last)
    for dy in (-1, 1):
        started.append(send_block(ld, dy, 0, HL, ny, nx, HL))
    loads[2].wait()
    pack_column(pack0, 0, 3, ms, HL, first)
    pack_column(pack0, 1, 3, ms, HL, last)
    for side, dx in ((0, -1), (1, 1)):
        started.append(send(pack0.at[side], land0.at[side], 0, dx))
    for dy in (-1, 1):
        started.append(send_block(ms, dy, 0, HL, ny, nx, HL))

    def coarse_row(rows, half, h, ref, y):
        tmp[h] = rows
        parts = [tmp[h, pl.ds(k, cx, stride=RATIO), :] for k in range(RATIO)]
        ref[HC + y, pl.ds(PAD, cx), half] = (
            (parts[0] + parts[1]) + (parts[2] + parts[3])
        ) * (1.0 / RATIO)

    def mass_row(y, carry):
        for h, half in enumerate(halves):
            rows = [ms[HL + y * RATIO + k, middle, half] for k in range(RATIO)]
            coarse_row((rows[0] + rows[1]) + (rows[2] + rows[3]), half, h, cm, y)
        return carry

    lax.fori_loop(0, cy, mass_row, 0)
    mass_sent = [send_block(cm, dy, dx, HC, cy, cx, HC) for dy, dx in around]

    for copy in started:
        copy.wait_recv()
    for k in range(2):
        unpack_column(land0, 1, k, u0, HU, PAD - 1 - k)
        unpack_column(land0, 0, k, u0, HU, PAD + nx + k)
    for at, ref in ((2, ld), (3, ms)):
        unpack_column(land0, 1, at, ref, HL, PAD - 1)
        unpack_column(land0, 0, at, ref, HL, PAD + nx)

    def weight_row(r, carry):
        for half in halves:
            wt[r, :, half] = 0.8 / (4.0 + ms[r, :, half])
        return carry

    lax.fori_loop(0, ny + 2 * HL, weight_row, 0)

    def neighbours(src, r, half, width):
        here = src[r, :, half]
        total = (
            src[r - 1, :, half] + src[r + 1, :, half]
            + pltpu.roll(here, 1, 0) + pltpu.roll(here, width - 1, 0)
        )
        return here, total

    def sweep_row(src, dst, y, columns=None):
        for half in halves:
            here, total = neighbours(src, HU + y, half, wide)
            new = 0.2 * here + wt[HL + y, :, half] * (ld[HL + y, :, half] + total)
            if columns is None:
                dst[HU + y, :, half] = new
            else:
                dst[HU + y, middle, half] = new[PAD : PAD + nx]

    def sweep(src, dst, begin, end, columns=None):
        def body(y, carry):
            sweep_row(src, dst, y, columns)
            return carry

        lax.fori_loop(begin, end, body, 0)

    sweep(u0, u1, -1, ny + 1)
    sweep(u1, u2, 0, ny, middle)

    for k in range(2):
        pack_column(pack1, 0, k, u2, HU, first + k)
        pack_column(pack1, 1, k, u2, HU, last - k)
    sent1 = [send(pack1.at[side], land1.at[side], 0, dx) for side, dx in ((0, -1), (1, 1))]
    for dy in (-1, 1):
        sent1.append(send_block(u2, dy, 0, HU, ny, nx, HU))
    for dy, dx in DIAGONALS:
        sent1.append(send_block(u2, dy, dx, HU, ny, nx, 1))
    for copy in sent1:
        copy.wait_recv()
    for k in range(2):
        unpack_column(land1, 1, k, u2, HU, PAD - 1 - k)
        unpack_column(land1, 0, k, u2, HU, PAD + nx + k)

    def defect_row(y, carry):
        for h, half in enumerate(halves):
            total = None
            for k in range(RATIO):
                r = y * RATIO + k
                here, beside = neighbours(u2, HU + r, half, wide)
                term = ld[HL + r, :, half] + beside - (4.0 + ms[HL + r, :, half]) * here
                total = term if total is None else total + term
            coarse_row(total[PAD : PAD + nx], half, h, cl, y)
        return carry

    lax.fori_loop(0, cy, defect_row, 0)

    sent2 = [send_block(cl, dy, dx, HC, cy, cx, HC) for dy, dx in around]
    for copy in mass_sent:
        copy.wait_recv()
    crows = cy + 2 * HC

    def coarse_weight(r, carry):
        for half in halves:
            cw[r, :, half] = 0.8 / (4.0 + cm[r, :, half])
        return carry

    lax.fori_loop(0, crows, coarse_weight, 0)
    for copy in sent2:
        copy.wait_recv()

    def coarse_first(r, carry):
        for half in halves:
            cva[r, :, half] = cw[r, :, half] * cl[r, :, half]
        return carry

    lax.fori_loop(0, crows, coarse_first, 0)
    src, dst = cva, cvb
    for step in range(1, INNER):

        def coarse_sweep(r, carry, src=src, dst=dst):
            for half in halves:
                here, total = neighbours(src, r, half, cwide)
                dst[r, :, half] = 0.2 * here + cw[r, :, half] * (cl[r, :, half] + total)
            return carry

        lax.fori_loop(step, crows - step, coarse_sweep, 0)
        src, dst = dst, src
    coarse = src

    begin = PAD - PAD // RATIO
    cells = wide // RATIO

    def correct(cell_row, rows):
        for h, half in enumerate(halves):
            cell = coarse[cell_row, pl.ds(begin, cells), half]
            for k in range(RATIO):
                spread[h, pl.ds(k, cells, stride=RATIO), :] = cell
            whole = spread[h]
            for r in rows:
                u0[r, :, half] = u2[r, :, half] + whole

    def correct_row(y, carry):
        correct(HC + y, [HU + y * RATIO + k for k in range(RATIO)])
        return carry

    for copy in started + mass_sent + sent1 + sent2:
        copy.wait_send()
    correct(HC - 1, list(range(HU)))
    lax.fori_loop(0, cy, correct_row, 0)
    correct(HC + cy, list(range(HU + ny, 2 * HU + ny)))

    sweep(u0, u1, -1, ny + 1)
    chunk = 8
    outs = []
    for c in range(ny // chunk):
        sweep(u1, u2, c * chunk, (c + 1) * chunk, middle)
        copy = pltpu.make_async_copy(
            u2.at[pl.ds(HU + c * chunk, chunk), middle],
            out_hbm.at[pl.ds(c * chunk, chunk)],
            out_sem.at[c],
        )
        copy.start()
        outs.append(copy)
    for copy in outs:
        copy.wait()


def solution(mesh):
    n_py, n_px = mesh.shape["py"], mesh.shape["px"]

    def per_device(load_terms, start_values, reaction_rate):
        ny, nx, members = load_terms.shape
        cy, cx = ny // RATIO, nx // RATIO
        wide, cwide = nx + 2 * PAD, cx + 2 * PAD
        fine = pltpu.VMEM((ny + 2 * HU, wide, members), jnp.float32)
        term = pltpu.VMEM((ny + 2 * HL, wide, members), jnp.float32)
        coarse = pltpu.VMEM((cy + 2 * HC, cwide, members), jnp.float32)
        columns0 = pltpu.VMEM((2, 4, ny // 8, 8, members), jnp.float32)
        columns1 = pltpu.VMEM((2, 2, ny // 8, 8, members), jnp.float32)
        copies = 36
        return pl.pallas_call(
            functools.partial(kernel, (ny, nx, members, n_py, n_px)),
            out_shape=jax.ShapeDtypeStruct(load_terms.shape, jnp.float32),
            in_specs=[pl.BlockSpec(memory_space=pltpu.HBM)] * 3,
            out_specs=pl.BlockSpec(memory_space=pltpu.HBM),
            scratch_shapes=[
                fine, fine, fine, term, term, term,
                coarse, coarse, coarse, coarse, coarse,
                columns0, columns1, columns0, columns1,
                pltpu.VMEM((members // LANES, nx, LANES), jnp.float32),
                pltpu.VMEM((members // LANES, wide, LANES), jnp.float32),
                pltpu.SemaphoreType.DMA((3,)),
                pltpu.SemaphoreType.DMA((ny // 8,)),
                pltpu.SemaphoreType.DMA((copies,)),
                pltpu.SemaphoreType.DMA((copies,)),
            ],
            compiler_params=pltpu.CompilerParams(
                collective_id=0, has_side_effects=True, vmem_limit_bytes=60 * 2**20
            ),
        )(load_terms, start_values, reaction_rate)

    spec = P("py", "px", None)
    return jax.shard_map(
        per_device, mesh=mesh, in_specs=(spec, spec, spec), out_specs=spec, check_vma=False
    )
```

time: 190 us -> 69 us (0.36)
  other arithmetic: 77.1 us -> 0 us
  Pallas kernels: 0 us -> 64.2 us
  starting transfers between devices: 60.1 us -> 0 us
  waiting for transfers between devices: 30.4 us -> 0 us
  local copies, waits for them, and re-layouts: 21.7 us -> 4.7 us
    pallas_call x0 -> x1, Pallas kernels: none -> 64.2 us  [per_device(): pl.pallas_call(functools.partial(kernel, (ny, nx, members, n_py, n_px)),...]
    ppermute x36 -> x0, starting transfers between devices: 60.1 us -> none  [the longest x18 52.9 us: extended(): after = lax.ppermute(leading, axis, down)]
    add x11 -> x0, other arithmetic: 54.4 us -> none  [the longest x10 51.6 us: relax_once(): values + 0.8 * (load + around_sum(padded) - (4.0 + mass_here) * values) /...]
    ppermute x36 -> x0, waiting for transfers between devices: 30.4 us -> none  [the longest x18 30.1 us: extended(): before = lax.ppermute(last, axis, up)]
    sub x1 -> x0, other arithmetic: 15 us -> none  [per_device(): load_terms + around_sum(extended(values, (('py', 0), ('px', 1)), 1))]
    reshape x3 -> x0, local copies, waits for them, and re-layouts: 10.8 us -> none  [the longest x2 10.4 us: block_means(): values.reshape(values.shape[0] // RATIO, RATIO, values.shape[1] // RATIO,...]
    reduce_sum x2 -> x0, other arithmetic: 7.09 us -> none  [block_means(): return jnp.mean(cut, axis=(1, 3))]
    add x1 -> x0, local copies, waits for them, and re-layouts: 4.44 us -> none  [relax_once(): values + 0.8 * (load + around_sum(padded) - (4.0 + mass_here) * values) /...]
  transfers between devices with their start and end apart: 36 -> 0, of which waited for: 15 -> 0; matrix products, arithmetic and copies ran while one was open for 7% -> 0% of each run, Pallas kernels for 0% -> 0%
where the time goes in v1:
time: 69 us; the launch traced here: 68.9 us
  Pallas kernels  64.2 us (93%)
  local copies, waits for them, and re-layouts  4.7 us (7%)
    pallas_call x1, Pallas kernels, per_device(): pl.pallas_call(functools.partial(kernel, (ny, nx, members, n_py, n_px)),...  64.2 us
    unnamed x1, local copies, waits for them, and re-layouts  4.7 us

profile of v1, /device:TPU:0, one launch (start us, length us, event | category | flops | bytes accessed | tf_op | source)
XLA Modules:
  0.0 68.9 jit_solution(11555173566607223052)
XLA Ops:
  0.0 64.2 %shard_map.37 = f32[64,64,256]{2,1,0:T(8,128)} custom-call(f32[64,64,256]{2,1,0:T(8,128)} %load_hbm.1, f32[64,64,256]{2,1,0:T(8,128)} %start_hbm.1, f32[64,64,256]{2,1,0:T(8,128)} %mass_hbm.1), custom_call_target="tpu_custom_call" | custom-call | tf_op jit(solution)/shard_map/pallas_call | solution.py:290
  64.2 4.7 %copy.5 = f32[64,64,256]{2,1,0:T(8,128)} copy(f32[64,64,256]{2,1,0:T(8,128)} %shard_map.37) | data formatting | bytes 8388608

commit v2 on v1

--- a/solution.py
+++ b/solution.py
@@ -100,6 +100,14 @@
     for k in range(2):
         pack_column(pack0, 0, k, u0, HU, first + k)
         pack_column(pack0, 1, k, u0, HU, last - k)
+    sides = ((0, -1), (1, 1))
+
+    def send_columns(at, length):
+        for side, dx in sides:
+            piece = pl.ds(at, length)
+            started.append(send(pack0.at[side, piece], land0.at[side, piece], 0, dx))
+
+    send_columns(0, 2)
     for dy in (-1, 1):
         started.append(send_block(u0, dy, 0, HU, ny, nx, HU))
     for dy, dx in DIAGONALS:
@@ -107,13 +115,13 @@
     loads[1].wait()
     pack_column(pack0, 0, 2, ld, HL, first)
     pack_column(pack0, 1, 2, ld, HL, last)
+    send_columns(2, 1)
     for dy in (-1, 1):
         started.append(send_block(ld, dy, 0, HL, ny, nx, HL))
     loads[2].wait()
     pack_column(pack0, 0, 3, ms, HL, first)
     pack_column(pack0, 1, 3, ms, HL, last)
-    for side, dx in ((0, -1), (1, 1)):
-        started.append(send(pack0.at[side], land0.at[side], 0, dx))
+    send_columns(3, 1)
     for dy in (-1, 1):
         started.append(send_block(ms, dy, 0, HL, ny, nx, HL))
 
@@ -133,6 +141,12 @@
     lax.fori_loop(0, cy, mass_row, 0)
     mass_sent = [send_block(cm, dy, dx, HC, cy, cx, HC) for dy, dx in around]
 
+    def weight_inside(r, carry):
+        for half in halves:
+            wt[r, middle, half] = 0.8 / (4.0 + ms[r, middle, half])
+        return carry
+
+    lax.fori_loop(HL, HL + ny, weight_inside, 0)
     for copy in started:
         copy.wait_recv()
     for k in range(2):
@@ -142,12 +156,16 @@
         unpack_column(land0, 1, at, ref, HL, PAD - 1)
         unpack_column(land0, 0, at, ref, HL, PAD + nx)
 
-    def weight_row(r, carry):
+    def weight_beside(r, carry):
+        for half in halves:
+            for columns in (pl.ds(0, PAD), pl.ds(PAD + nx, PAD)):
+                wt[r, columns, half] = 0.8 / (4.0 + ms[r, columns, half])
+        return carry
+
+    lax.fori_loop(HL, HL + ny, weight_beside, 0)
+    for r in (0, HL + ny):
         for half in halves:
             wt[r, :, half] = 0.8 / (4.0 + ms[r, :, half])
-        return carry
-
-    lax.fori_loop(0, ny + 2 * HL, weight_row, 0)
 
     def neighbours(src, r, half, width):
         here = src[r, :, half]
@@ -286,7 +304,7 @@
         coarse = pltpu.VMEM((cy + 2 * HC, cwide, members), jnp.float32)
         columns0 = pltpu.VMEM((2, 4, ny // 8, 8, members), jnp.float32)
         columns1 = pltpu.VMEM((2, 2, ny // 8, 8, members), jnp.float32)
-        copies = 36
+        copies = 40
         return pl.pallas_call(
             functools.partial(kernel, (ny, nx, members, n_py, n_px)),
             out_shape=jax.ShapeDtypeStruct(load_terms.shape, jnp.float32),

time: 69 us -> 68.2 us (0.988)
  Pallas kernels: 64.2 us -> 63.4 us
    pallas_call x1, Pallas kernels: 64.2 us -> 63.4 us  [per_device(): pl.pallas_call(functools.partial(kernel, (ny, nx, members, n_py, n_px)),...]
where the time goes in v2:
time: 68.2 us; the launch traced here: 68.1 us
  Pallas kernels  63.4 us (93%)
  local copies, waits for them, and re-layouts  4.7 us (7%)
    pallas_call x1, Pallas kernels, per_device(): pl.pallas_call(functools.partial(kernel, (ny, nx, members, n_py, n_px)),...  63.4 us
    unnamed x1, local copies, waits for them, and re-layouts  4.7 us

profile of v2, /device:TPU:0, one launch (start us, length us, event | category | flops | bytes accessed | tf_op | source)
XLA Modules:
  0.0 68.1 jit_solution(13284549745314127080)
XLA Ops:
  0.0 63.4 %shard_map.37 = f32[64,64,256]{2,1,0:T(8,128)} custom-call(f32[64,64,256]{2,1,0:T(8,128)} %load_hbm.1, f32[64,64,256]{2,1,0:T(8,128)} %start_hbm.1, f32[64,64,256]{2,1,0:T(8,128)} %mass_hbm.1), custom_call_target="tpu_custom_call" | custom-call | tf_op jit(solution)/shard_map/pallas_call | solution.py:308
  63.4 4.7 %copy.5 = f32[64,64,256]{2,1,0:T(8,128)} copy(f32[64,64,256]{2,1,0:T(8,128)} %shard_map.37) | data formatting | bytes 8388608

commit v3 on v2

--- a/solution.py
+++ b/solution.py
@@ -192,16 +192,33 @@
         lax.fori_loop(begin, end, body, 0)
 
     sweep(u0, u1, -1, ny + 1)
-    sweep(u1, u2, 0, ny, middle)
-
+    sweep(u1, u2, 0, HU, middle)
+    sweep(u1, u2, ny - HU, ny, middle)
+    sent1 = []
+    for dy, dx in DIAGONALS:
+        sent1.append(send_block(u2, dy, dx, HU, ny, nx, 1))
+    for dy in (-1, 1):
+        sent1.append(send_block(u2, dy, 0, HU, ny, nx, HU))
+
+    def outer_columns(y, carry):
+        for half in halves:
+            for begin, at in ((0, PAD), (nx, 0)):
+                window = pl.ds(begin, 2 * PAD)
+                here = u1[HU + y, window, half]
+                total = (
+                    u1[HU + y - 1, window, half] + u1[HU + y + 1, window, half]
+                    + pltpu.roll(here, 1, 0) + pltpu.roll(here, 2 * PAD - 1, 0)
+                )
+                new = 0.2 * here + wt[HL + y, window, half] * (ld[HL + y, window, half] + total)
+                u2[HU + y, pl.ds(begin + at, PAD), half] = new[at : at + PAD]
+        return carry
+
+    lax.fori_loop(HU, ny - HU, outer_columns, 0)
     for k in range(2):
         pack_column(pack1, 0, k, u2, HU, first + k)
         pack_column(pack1, 1, k, u2, HU, last - k)
-    sent1 = [send(pack1.at[side], land1.at[side], 0, dx) for side, dx in ((0, -1), (1, 1))]
-    for dy in (-1, 1):
-        sent1.append(send_block(u2, dy, 0, HU, ny, nx, HU))
-    for dy, dx in DIAGONALS:
-        sent1.append(send_block(u2, dy, dx, HU, ny, nx, 1))
+    sent1 += [send(pack1.at[side], land1.at[side], 0, dx) for side, dx in sides]
+    sweep(u1, u2, HU, ny - HU, middle)
     for copy in sent1:
         copy.wait_recv()
     for k in range(2):

time: 68.2 us -> 65.1 us (0.955)
  Pallas kernels: 63.4 us -> 60.3 us
    pallas_call x1, Pallas kernels: 63.4 us -> 60.3 us  [per_device(): pl.pallas_call(functools.partial(kernel, (ny, nx, members, n_py, n_px)),...]
where the time goes in v3:
time: 65.1 us; the launch traced here: 65 us
  Pallas kernels  60.3 us (93%)
  local copies, waits for them, and re-layouts  4.7 us (7%)
    pallas_call x1, Pallas kernels, per_device(): pl.pallas_call(functools.partial(kernel, (ny, nx, members, n_py, n_px)),...  60.3 us
    unnamed x1, local copies, waits for them, and re-layouts  4.7 us

profile of v3, /device:TPU:0, one launch (start us, length us, event | category | flops | bytes accessed | tf_op | source)
XLA Modules:
  0.0 65.0 jit_solution(18048721737481131979)
XLA Ops:
  0.0 60.3 %shard_map.37 = f32[64,64,256]{2,1,0:T(8,128)} custom-call(f32[64,64,256]{2,1,0:T(8,128)} %load_hbm.1, f32[64,64,256]{2,1,0:T(8,128)} %start_hbm.1, f32[64,64,256]{2,1,0:T(8,128)} %mass_hbm.1), custom_call_target="tpu_custom_call" | custom-call | tf_op jit(solution)/shard_map/pallas_call | solution.py:325
  60.3 4.7 %copy.5 = f32[64,64,256]{2,1,0:T(8,128)} copy(f32[64,64,256]{2,1,0:T(8,128)} %shard_map.37) | data formatting | bytes 8388608
